TPU v7x, 32 devices: a whole 2x2x4 slice. The times are simulated.
32 devices in a mesh: gx: 4 (over z), gy: 2 (over x), gz: 4 (over y, core).
Axes of the slice: x: 2, y: 2, z: 4, core: 2. Of those that a mesh axis runs over, the one named last changes fastest.
Arguments:
- bases: float32 [4, 2, 4, 1024, 128], P('gx', 'gy', 'gz'), may hold values from -1 to 1, as said below
- ranks: int32 [4, 2, 4], P('gx', 'gy', 'gz'), may hold values from 64 to 128
- couplings: bfloat16 [4, 2, 4, 5, 1024, 1024], P('gx', 'gy', 'gz'), may hold values from -6 to 6
- vectors: float32 [4, 2, 4, 1024, 256], P('gx', 'gy', 'gz'), may hold values from -0.1875 to 0.1875
Outputs:
- projected: float32 [4, 2, 4, 5, 128, 128], P('gx', 'gy', 'gz')
- applied: float32 [4, 2, 4, 1024, 256], P('gx', 'gy', 'gz')
Inputs may be any that keep to these rules, and one draw needn't show every extreme that they name: `bases`: for each subdomain the 1024 x 128 matrix has orthonormal columns.
All inputs are finite; a program needn't handle non-finite values.
Results may differ from a plain program's by a relative error of at most 0.0003.
Values sent between devices are 32-bit elements; how exact they have to be, the bound alone decides.
A program may use at most 64 MiB of HBM per device.

v0:
```python
import functools

import jax
import jax.numpy as jnp
from jax import lax
from jax.experimental import pallas as pl
from jax.experimental.pallas import tpu as pltpu
from jax.sharding import PartitionSpec as P

OFFSET_LIST = ((1, 0, 0), (0, 1, 0), (0, 0, 1), (1, 1, 0), (1, 0, 1), (0, 1, 1), (1, 1, 1))
AXES = ("gx", "gy", "gz")
X, Y, Z, XY, XZ = range(5)
LEFT_ORDER = (XY, Y, X, XZ, Z)


def split2(value):
    high = value.astype(jnp.bfloat16)
    low = (value - high.astype(jnp.float32)).astype(jnp.bfloat16)
    return high, low


def dot32(left, right):
    return jnp.dot(left, right, preferred_element_type=jnp.float32)


def kernel(
    sizes, ranks_ref, bases_ref, couplings_ref, vectors_ref, projected_ref, applied_ref,
    basis, stacked, basis_parts, blocks, values, left_out, left_in, relay, back_out, back_in,
    basis_sem, block_sem, value_send, value_recv, left_send, left_recv, relay_send, relay_recv, back_send, back_recv,
):
    count, m, k = blocks.shape[0], basis.shape[0], basis.shape[1]
    r = applied_ref.shape[1]
    half = m // 2
    place = [lax.axis_index(name) for name in AXES]
    has_up = [p < n - 1 for p, n in zip(place, sizes)]
    has_down = [p > 0 for p in place]

    def every(flags, offset):
        out = None
        for flag, o in zip(flags, offset):
            if o:
                out = flag if out is None else jnp.logical_and(out, flag)
        return out

    up = [every(has_up, o) for o in OFFSET_LIST[:count]]
    down = [every(has_down, o) for o in OFFSET_LIST[:count]]

    def device(offset, sign):
        return {name: p + sign * o for name, p, o in zip(AXES, place, offset)}

    basis_copy = pltpu.make_async_copy(bases_ref, basis, basis_sem)
    basis_copy.start()
    block_copies = [
        pltpu.make_async_copy(couplings_ref.at[s], blocks.at[s], block_sem.at[s]) for s in range(count)
    ]
    for s in LEFT_ORDER:
        block_copies[s].start()

    barrier = pltpu.get_barrier_semaphore()
    partners = jnp.int32(0)
    for s in range(count):
        for flag, sign in ((up[s], 1), (down[s], -1)):
            partners = partners + flag.astype(jnp.int32)

            @pl.when(flag)
            def _():
                pl.semaphore_signal(
                    barrier, inc=1, device_id=device(OFFSET_LIST[s], sign), device_id_type=pl.DeviceIdType.MESH
                )

    pl.semaphore_wait(barrier, partners)

    def rows(part):
        return pl.ds(part * half, half)

    def remote(src, dst, send, recv, offset, sign):
        return pltpu.make_async_remote_copy(
            src_ref=src, dst_ref=dst, send_sem=send, recv_sem=recv,
            device_id=device(offset, sign), device_id_type=pl.DeviceIdType.MESH,
        )

    def value_copy(slot, part, source, offset):
        return remote(
            source.at[rows(part)], values.at[slot, rows(part)],
            value_send.at[slot, part], value_recv.at[slot, part], offset, -1,
        )

    sent = {}
    for s in (X, Y, Z):
        for part in (0, 1):
            sent[s, part] = (value_copy(s, part, vectors_ref, OFFSET_LIST[s]), down[s])
    sent[XY, 0] = (value_copy(XY, 0, values.at[X], OFFSET_LIST[Y]), jnp.logical_and(has_up[0], has_down[1]))
    sent[XY, 1] = (value_copy(XY, 1, values.at[Y], OFFSET_LIST[X]), jnp.logical_and(has_up[1], has_down[0]))
    for part in (0, 1):
        sent[XZ, part] = (
            value_copy(XZ, part, values.at[X], OFFSET_LIST[Z]), jnp.logical_and(has_up[0], has_down[2]),
        )

    def start(slot, part):
        copy, flag = sent[slot, part]
        pl.when(flag)(copy.start)

    def arrived(slot, part):
        pl.when(up[slot])(sent[slot, part][0].wait_recv)

    relays = [
        remote(left_out.at[XY, part], relay.at[part], relay_send.at[part], relay_recv.at[part], OFFSET_LIST[s], 1)
        for part, s in ((0, X), (1, Y))
    ]
    onward = [
        remote(relay.at[part], left_in.at[XY, part], left_send.at[XY, part], left_recv.at[XY, part], OFFSET_LIST[s], 1)
        for part, s in ((0, Y), (1, X))
    ]
    passed = (
        ((relays[0], onward[0]), jnp.logical_and(has_down[0], has_up[1])),
        ((relays[1], onward[1]), jnp.logical_and(has_down[1], has_up[0])),
    )
    left_copies = [
        relays if s == XY else [
            remote(left_out.at[s], left_in.at[s], left_send.at[s, 0], left_recv.at[s, 0], OFFSET_LIST[s], 1)
        ]
        for s in range(count)
    ]
    back_copies = [
        remote(back_out.at[s], back_in.at[s], back_send.at[s], back_recv.at[s], OFFSET_LIST[s], -1)
        for s in range(count)
    ]

    start(X, 0)
    start(Y, 1)
    start(Z, 0)
    start(X, 1)
    start(Y, 0)
    start(Z, 1)

    basis_copy.wait()
    columns = lax.broadcasted_iota(jnp.int32, (m, k), 1)
    masked = jnp.where(columns < ranks_ref[0, 0, 0], basis[...], 0.0)
    high, low = split2(masked)
    basis_parts[:, :k] = high
    basis_parts[:, k:] = low
    high, low = split2(masked.T)
    stacked[:k] = high
    stacked[k:] = low

    for s in LEFT_ORDER:
        block_copies[s].wait()

        @pl.when(up[s])
        def _():
            @pl.loop(0, 2)
            def _(part):
                there = pl.ds(pl.multiple_of(part * half, half), half)
                both = dot32(stacked[...], blocks[s, :, there])
                left_out[s, part] = both[:k] + both[k:]

            for copy in left_copies[s]:
                copy.start()

    applied_ref[...] = jnp.zeros_like(applied_ref)
    for s in range(count):

        @pl.when(jnp.logical_not(up[s]))
        def _():
            back_in[s] = jnp.zeros((k, k), jnp.float32)

    for copy, flag in passed:
        @pl.when(flag)
        def _():
            copy[0].wait_recv()
            copy[1].start()

    tall = min(512, m)

    def apply(slot, part):
        @pl.when(up[slot])
        def _():
            high, low = split2(values[slot, rows(part)])
            pair = jnp.concatenate([high, low], axis=1)

            @pl.loop(0, m // tall)
            def _(step):
                there = pl.ds(pl.multiple_of(step * tall, tall), tall)
                both = dot32(blocks[slot, there, rows(part)], pair)
                applied_ref[there] += both[:, :r] + both[:, r:]

    def project(slot):
        @pl.when(down[slot])
        def _():
            for copy in onward if slot == XY else left_copies[slot]:
                copy.wait_recv()
            out = None
            for part in (0, 1):
                high, low = split2(left_in[slot, part])
                first = dot32(high, basis_parts[rows(part)])
                term = first[:, :k] + first[:, k:] + dot32(low, basis_parts[rows(part), :k])
                out = term if out is None else out + term
            back_out[slot] = out
            back_copies[slot].start()

    arrived(X, 0)
    start(XY, 0)
    start(XZ, 0)
    arrived(Y, 1)
    start(XY, 1)
    arrived(Z, 0)
    arrived(Z, 1)
    apply(Z, 0)
    apply(Z, 1)
    apply(X, 0)
    apply(Y, 1)
    project(Z)
    project(Y)
    project(XY)
    arrived(X, 1)
    start(XZ, 1)
    arrived(Y, 0)
    apply(X, 1)
    apply(Y, 0)
    arrived(XZ, 0)
    apply(XZ, 0)
    project(X)
    arrived(XZ, 1)
    apply(XZ, 1)
    project(XZ)
    arrived(XY, 0)
    apply(XY, 0)
    arrived(XY, 1)
    apply(XY, 1)
    for s in range(count):
        pl.when(up[s])(back_copies[s].wait_recv)
    projected_ref[...] = back_in[...]
    for s in range(count):
        for part in (0, 1):
            copy, flag = sent[s, part]
            pl.when(flag)(copy.wait_send)
        for copy in left_copies[s]:
            pl.when(up[s])(copy.wait_send)
        pl.when(down[s])(back_copies[s].wait_send)
    for copy, flag in passed:
        pl.when(flag)(copy[1].wait_send)


def solution(mesh):
    sizes = tuple(mesh.shape[name] for name in AXES)

    def local(bases, ranks, couplings, vectors):
        m, k = bases.shape[-2:]
        count = couplings.shape[3]
        r = vectors.shape[-1]
        f32, bf16 = jnp.float32, jnp.bfloat16
        dma = pltpu.SemaphoreType.DMA
        projected, applied = pl.pallas_call(
            functools.partial(kernel, sizes),
            out_shape=(
                pltpu.VMEM((count, k, k), f32),
                pltpu.VMEM((m, r), f32),
            ),
            in_specs=[pl.BlockSpec(memory_space=pltpu.SMEM)] + [pl.BlockSpec(memory_space=pltpu.HBM)] * 3,
            out_specs=(pl.BlockSpec(memory_space=pltpu.VMEM),) * 2,
            scratch_shapes=[
                pltpu.VMEM((m, k), f32),
                pltpu.VMEM((2 * k, m), bf16),
                pltpu.VMEM((m, 2 * k), bf16),
                pltpu.VMEM((count, m, m), bf16),
                pltpu.VMEM((count, m, r), f32),
                pltpu.VMEM((count, 2, k, m // 2), f32),
                pltpu.VMEM((count, 2, k, m // 2), f32),
                pltpu.VMEM((2, k, m // 2), f32),
                pltpu.VMEM((count, k, k), f32),
                pltpu.VMEM((count, k, k), f32),
                dma,
                dma((count,)),
                dma((count, 2)),
                dma((count, 2)),
                dma((count, 2)),
                dma((count, 2)),
                dma((2,)),
                dma((2,)),
                dma((count,)),
                dma((count,)),
            ],
            compiler_params=pltpu.CompilerParams(collective_id=0, has_side_effects=True, vmem_limit_bytes=64000 << 10),
        )(
            ranks,
            bases.reshape(m, k),
            couplings.reshape(count, m, m),
            vectors.reshape(m, r),
        )
        return (
            projected.reshape(1, 1, 1, count, k, k),
            applied.reshape(1, 1, 1, m, r),
        )

    return jax.shard_map(
        local,
        mesh=mesh,
        in_specs=(
            P("gx", "gy", "gz", None, None),
            P("gx", "gy", "gz"),
            P("gx", "gy", "gz", None, None, None),
            P("gx", "gy", "gz", None, None),
        ),
        out_specs=(P("gx", "gy", "gz", None, None, None), P("gx", "gy", "gz", None, None)),
        check_vma=False,
    )
```

profile of v0, /device:TPU:0, one launch (start us, length us, event | category | flops | bytes accessed | tf_op | source)
XLA Modules:
  0.0 46.6 jit_solution(819324025144111263)
XLA Ops:
  1.3 43.6 %shard_map.59 = (f32[5,128,128]{2,1,0:T(8,128)S(1)}, f32[1024,256]{1,0:T(8,128)S(1)}) custom-call(s32[1,1,1]{2,1,0:T(1,128)S(6)} %copy.10.ranks_ref, f32[1024,128]{1,0:T(8,128)} %bitcast.9, bf16[5,1024,1024]{2,1,0:T(8,128)(2,1)} %bitcast.7, f32[1024,256]{1,0:T(8,128)} %bitcast.8), custom_call_target="tpu_custom_call" | custom-call | tf_op jit(solution)/shard_map/pallas_call | solution.py:253
  44.9 0.7 %copy.8 = f32[1,1,1,5,128,128]{5,4,3,2,1,0:T(8,128)} copy(f32[1,1,1,5,128,128]{5,4,3,2,1,0:T(8,128)S(1)} %bitcast.6) | data formatting | bytes 655360
  45.6 1.0 %copy.9 = f32[1,1,1,1024,256]{4,3,2,1,0:T(8,128)} copy(f32[1,1,1,1024,256]{4,3,2,1,0:T(8,128)S(1)} %bitcast.5) | data formatting | bytes 2097152
where the time goes:
time: 47.2 us; the launch traced here: 46.6 us
  Pallas kernels  43.6 us (92%)
  local copies, waits for them, and re-layouts  1.7 us (4%)
  between operations  1.28 us (3%)
    pallas_call x1, Pallas kernels, local(): pl.pallas_call(functools.partial(kernel, sizes), out_shape=(pltpu.VMEM((c...  43.6 us
    unnamed x2, local copies, waits for them, and re-layouts  1.7 us

commit v1 on v0

--- a/solution.py
+++ b/solution.py
@@ -11,6 +11,7 @@
 AXES = ("gx", "gy", "gz")
 X, Y, Z, XY, XZ = range(5)
 LEFT_ORDER = (XY, Y, X, XZ, Z)
+LEFT_SLOTS = (X, Y, Z, XZ)
 
 
 def split2(value):
@@ -25,8 +26,9 @@
 
 def kernel(
     sizes, ranks_ref, bases_ref, couplings_ref, vectors_ref, projected_ref, applied_ref,
-    basis, stacked, basis_parts, blocks, values, left_out, left_in, relay, back_out, back_in,
-    basis_sem, block_sem, value_send, value_recv, left_send, left_recv, relay_send, relay_recv, back_send, back_recv,
+    basis, stacked, basis_parts, blocks, values, left_out, left_in, relay, back_out,
+    ready, basis_sem, block_sem, value_send, value_recv, left_send, left_recv, relay_send, relay_recv,
+    back_send, back_recv,
 ):
     count, m, k = blocks.shape[0], basis.shape[0], basis.shape[1]
     r = applied_ref.shape[1]
@@ -48,27 +50,20 @@
     def device(offset, sign):
         return {name: p + sign * o for name, p, o in zip(AXES, place, offset)}
 
-    basis_copy = pltpu.make_async_copy(bases_ref, basis, basis_sem)
-    basis_copy.start()
-    block_copies = [
-        pltpu.make_async_copy(couplings_ref.at[s], blocks.at[s], block_sem.at[s]) for s in range(count)
-    ]
-    for s in LEFT_ORDER:
-        block_copies[s].start()
-
     barrier = pltpu.get_barrier_semaphore()
     partners = jnp.int32(0)
     for s in range(count):
-        for flag, sign in ((up[s], 1), (down[s], -1)):
-            partners = partners + flag.astype(jnp.int32)
-
-            @pl.when(flag)
-            def _():
-                pl.semaphore_signal(
-                    barrier, inc=1, device_id=device(OFFSET_LIST[s], sign), device_id_type=pl.DeviceIdType.MESH
-                )
-
-    pl.semaphore_wait(barrier, partners)
+        partners = partners + down[s].astype(jnp.int32)
+
+        @pl.when(up[s])
+        def _():
+            pl.semaphore_signal(
+                barrier, inc=1, device_id=device(OFFSET_LIST[s], 1), device_id_type=pl.DeviceIdType.MESH
+            )
+
+    @pl.when(partners > 0)
+    def _():
+        pl.semaphore_wait(barrier, partners)
 
     def rows(part):
         return pl.ds(part * half, half)
@@ -79,29 +74,36 @@
             device_id=device(offset, sign), device_id_type=pl.DeviceIdType.MESH,
         )
 
-    def value_copy(slot, part, source, offset):
+    def value_copy(slot, piece, source, offset):
         return remote(
-            source.at[rows(part)], values.at[slot, rows(part)],
-            value_send.at[slot, part], value_recv.at[slot, part], offset, -1,
+            source.at[piece], values.at[slot, piece],
+            value_send.at[slot, len(sent[slot])], value_recv.at[slot, len(sent[slot])], offset, -1,
         )
 
-    sent = {}
+    def pieces(part, total):
+        return [pl.ds(part * half + p * (half // total), half // total) for p in range(total)]
+
+    sent = {s: [] for s in range(count)}
+
+    def plan(slot, part, source, offset, flag, total=1):
+        for piece in pieces(part, total):
+            sent[slot].append((value_copy(slot, piece, source, offset), piece, flag, part))
+
     for s in (X, Y, Z):
         for part in (0, 1):
-            sent[s, part] = (value_copy(s, part, vectors_ref, OFFSET_LIST[s]), down[s])
-    sent[XY, 0] = (value_copy(XY, 0, values.at[X], OFFSET_LIST[Y]), jnp.logical_and(has_up[0], has_down[1]))
-    sent[XY, 1] = (value_copy(XY, 1, values.at[Y], OFFSET_LIST[X]), jnp.logical_and(has_up[1], has_down[0]))
+            plan(s, part, vectors_ref, OFFSET_LIST[s], down[s])
+    plan(XY, 0, values.at[X], OFFSET_LIST[Y], jnp.logical_and(has_up[0], has_down[1]), 2)
+    plan(XY, 1, values.at[Y], OFFSET_LIST[X], jnp.logical_and(has_up[1], has_down[0]), 2)
     for part in (0, 1):
-        sent[XZ, part] = (
-            value_copy(XZ, part, values.at[X], OFFSET_LIST[Z]), jnp.logical_and(has_up[0], has_down[2]),
-        )
+        plan(XZ, part, values.at[X], OFFSET_LIST[Z], jnp.logical_and(has_up[0], has_down[2]))
 
     def start(slot, part):
-        copy, flag = sent[slot, part]
-        pl.when(flag)(copy.start)
-
-    def arrived(slot, part):
-        pl.when(up[slot])(sent[slot, part][0].wait_recv)
+        for copy, _, flag, its in sent[slot]:
+            if its == part:
+                pl.when(flag)(copy.start)
+
+    def arrived(slot, n):
+        pl.when(up[slot])(sent[slot][n][0].wait_recv)
 
     relays = [
         remote(left_out.at[XY, part], relay.at[part], relay_send.at[part], relay_recv.at[part], OFFSET_LIST[s], 1)
@@ -122,7 +124,7 @@
         for s in range(count)
     ]
     back_copies = [
-        remote(back_out.at[s], back_in.at[s], back_send.at[s], back_recv.at[s], OFFSET_LIST[s], -1)
+        remote(back_out.at[s], projected_ref.at[s], back_send.at[s], back_recv.at[s], OFFSET_LIST[s], -1)
         for s in range(count)
     ]
 
@@ -132,6 +134,21 @@
     start(X, 1)
     start(Y, 0)
     start(Z, 1)
+
+    for s in LEFT_SLOTS:
+        @pl.when(down[s])
+        def _():
+            pl.semaphore_signal(
+                ready.at[s], inc=1, device_id=device(OFFSET_LIST[s], -1), device_id_type=pl.DeviceIdType.MESH
+            )
+
+    basis_copy = pltpu.make_async_copy(bases_ref, basis, basis_sem)
+    basis_copy.start()
+    block_copies = [
+        pltpu.make_async_copy(couplings_ref.at[s], blocks.at[s], block_sem.at[s]) for s in range(count)
+    ]
+    for s in LEFT_ORDER:
+        block_copies[s].start()
 
     basis_copy.wait()
     columns = lax.broadcasted_iota(jnp.int32, (m, k), 1)
@@ -143,6 +160,11 @@
     stacked[:k] = high
     stacked[k:] = low
 
+    for s in LEFT_SLOTS:
+        @pl.when(up[s])
+        def _():
+            pl.semaphore_wait(ready.at[s], 1)
+
     for s in LEFT_ORDER:
         block_copies[s].wait()
 
@@ -154,15 +176,16 @@
                 both = dot32(stacked[...], blocks[s, :, there])
                 left_out[s, part] = both[:k] + both[k:]
 
-            for copy in left_copies[s]:
-                copy.start()
+            if s != XZ:
+                for copy in left_copies[s]:
+                    copy.start()
 
     applied_ref[...] = jnp.zeros_like(applied_ref)
     for s in range(count):
 
         @pl.when(jnp.logical_not(up[s]))
         def _():
-            back_in[s] = jnp.zeros((k, k), jnp.float32)
+            projected_ref[s] = jnp.zeros((k, k), jnp.float32)
 
     for copy, flag in passed:
         @pl.when(flag)
@@ -170,18 +193,22 @@
             copy[0].wait_recv()
             copy[1].start()
 
+    pl.when(up[XZ])(left_copies[XZ][0].start)
+
     tall = min(512, m)
 
-    def apply(slot, part):
+    def apply(slot, n):
+        piece = sent[slot][n][1]
+
         @pl.when(up[slot])
         def _():
-            high, low = split2(values[slot, rows(part)])
+            high, low = split2(values[slot, piece])
             pair = jnp.concatenate([high, low], axis=1)
 
             @pl.loop(0, m // tall)
             def _(step):
                 there = pl.ds(pl.multiple_of(step * tall, tall), tall)
-                both = dot32(blocks[slot, there, rows(part)], pair)
+                both = dot32(blocks[slot, there, piece], pair)
                 applied_ref[there] += both[:, :r] + both[:, r:]
 
     def project(slot):
@@ -198,47 +225,58 @@
             back_out[slot] = out
             back_copies[slot].start()
 
+    arrived(Z, 0)
+    apply(Z, 0)
     arrived(X, 0)
     start(XY, 0)
     start(XZ, 0)
     arrived(Y, 1)
     start(XY, 1)
-    arrived(Z, 0)
     arrived(Z, 1)
-    apply(Z, 0)
     apply(Z, 1)
     apply(X, 0)
     apply(Y, 1)
     project(Z)
+    arrived(XZ, 0)
+    apply(XZ, 0)
     project(Y)
-    project(XY)
+    project(X)
     arrived(X, 1)
     start(XZ, 1)
     arrived(Y, 0)
     apply(X, 1)
     apply(Y, 0)
-    arrived(XZ, 0)
-    apply(XZ, 0)
-    project(X)
     arrived(XZ, 1)
     apply(XZ, 1)
+    project(XY)
+    for n in (0, 2):
+        arrived(XY, n)
+        apply(XY, n)
     project(XZ)
-    arrived(XY, 0)
-    apply(XY, 0)
-    arrived(XY, 1)
-    apply(XY, 1)
+    for n in (1, 3):
+        arrived(XY, n)
+        apply(XY, n)
     for s in range(count):
         pl.when(up[s])(back_copies[s].wait_recv)
-    projected_ref[...] = back_in[...]
     for s in range(count):
-        for part in (0, 1):
-            copy, flag = sent[s, part]
+        for copy, _, flag, _ in sent[s]:
             pl.when(flag)(copy.wait_send)
         for copy in left_copies[s]:
             pl.when(up[s])(copy.wait_send)
         pl.when(down[s])(back_copies[s].wait_send)
     for copy, flag in passed:
         pl.when(flag)(copy[1].wait_send)
+
+
+def writer(projected_ref, applied_ref, projected_out, applied_out, sems):
+    copies = [
+        pltpu.make_async_copy(projected_ref, projected_out, sems.at[0]),
+        pltpu.make_async_copy(applied_ref, applied_out, sems.at[1]),
+    ]
+    for copy in copies:
+        copy.start()
+    for copy in copies:
+        copy.wait()
 
 
 def solution(mesh):
@@ -268,11 +306,11 @@
                 pltpu.VMEM((count, 2, k, m // 2), f32),
                 pltpu.VMEM((2, k, m // 2), f32),
                 pltpu.VMEM((count, k, k), f32),
-                pltpu.VMEM((count, k, k), f32),
+                pltpu.SemaphoreType.REGULAR((count,)),
                 dma,
                 dma((count,)),
-                dma((count, 2)),
-                dma((count, 2)),
+                dma((count, 4)),
+                dma((count, 4)),
                 dma((count, 2)),
                 dma((count, 2)),
                 dma((2,)),

time: 47.2 us -> 46.1 us (0.977)
  Pallas kernels: 43.6 us -> 43 us
    pallas_call x1, Pallas kernels: 43.6 us -> 43 us  [local(): pl.pallas_call(functools.partial(kernel, sizes), out_shape=(pltpu.VMEM((c...]
where the time goes in v1:
time: 46.1 us; the launch traced here: 45.9 us
  Pallas kernels  43 us (93%)
  local copies, waits for them, and re-layouts  1.7 us (4%)
  between operations  1.28 us (3%)
    pallas_call x1, Pallas kernels, local(): pl.pallas_call(functools.partial(kernel, sizes), out_shape=(pltpu.VMEM((c...  43 us
    unnamed x2, local copies, waits for them, and re-layouts  1.7 us

profile of v1, /device:TPU:0, one launch (start us, length us, event | category | flops | bytes accessed | tf_op | source)
XLA Modules:
  0.0 45.9 jit_solution(14199657324306947670)
XLA Ops:
  1.3 43.0 %shard_map.59 = (f32[5,128,128]{2,1,0:T(8,128)S(1)}, f32[1024,256]{1,0:T(8,128)S(1)}) custom-call(s32[1,1,1]{2,1,0:T(1,128)S(6)} %copy.10.ranks_ref, f32[1024,128]{1,0:T(8,128)} %bitcast.9, bf16[5,1024,1024]{2,1,0:T(8,128)(2,1)} %bitcast.7, f32[1024,256]{1,0:T(8,128)} %bitcast.8), custom_call_target="tpu_custom_call" | custom-call | tf_op jit(solution)/shard_map/pallas_call | solution.py:291
  44.2 0.7 %copy.8 = f32[1,1,1,5,128,128]{5,4,3,2,1,0:T(8,128)} copy(f32[1,1,1,5,128,128]{5,4,3,2,1,0:T(8,128)S(1)} %bitcast.6) | data formatting | bytes 655360
  45.0 1.0 %copy.9 = f32[1,1,1,1024,256]{4,3,2,1,0:T(8,128)} copy(f32[1,1,1,1024,256]{4,3,2,1,0:T(8,128)S(1)} %bitcast.5) | data formatting | bytes 2097152

commit v2 on v1

--- a/solution.py
+++ b/solution.py
@@ -50,6 +50,9 @@
     def device(offset, sign):
         return {name: p + sign * o for name, p, o in zip(AXES, place, offset)}
 
+    basis_copy = pltpu.make_async_copy(bases_ref, basis, basis_sem)
+    basis_copy.start()
+
     barrier = pltpu.get_barrier_semaphore()
     partners = jnp.int32(0)
     for s in range(count):
@@ -80,26 +83,28 @@
             value_send.at[slot, len(sent[slot])], value_recv.at[slot, len(sent[slot])], offset, -1,
         )
 
-    def pieces(part, total):
-        return [pl.ds(part * half + p * (half // total), half // total) for p in range(total)]
-
     sent = {s: [] for s in range(count)}
 
-    def plan(slot, part, source, offset, flag, total=1):
-        for piece in pieces(part, total):
+    def plan(slot, part, source, offset, flag, cuts=(1,)):
+        first = part * half
+        for cut in cuts:
+            piece = pl.ds(first, half // cut)
             sent[slot].append((value_copy(slot, piece, source, offset), piece, flag, part))
+            first += half // cut
 
     for s in (X, Y, Z):
         for part in (0, 1):
             plan(s, part, vectors_ref, OFFSET_LIST[s], down[s])
-    plan(XY, 0, values.at[X], OFFSET_LIST[Y], jnp.logical_and(has_up[0], has_down[1]), 2)
-    plan(XY, 1, values.at[Y], OFFSET_LIST[X], jnp.logical_and(has_up[1], has_down[0]), 2)
+    plan(XY, 0, values.at[X], OFFSET_LIST[Y], jnp.logical_and(has_up[0], has_down[1]), (2, 2))
+    plan(XY, 1, values.at[Y], OFFSET_LIST[X], jnp.logical_and(has_up[1], has_down[0]), (2, 4, 4))
     for part in (0, 1):
         plan(XZ, part, values.at[X], OFFSET_LIST[Z], jnp.logical_and(has_up[0], has_down[2]))
 
+    last = sent[XY][-1]
+
     def start(slot, part):
         for copy, _, flag, its in sent[slot]:
-            if its == part:
+            if its == part and copy is not last[0]:
                 pl.when(flag)(copy.start)
 
     def arrived(slot, n):
@@ -142,8 +147,6 @@
                 ready.at[s], inc=1, device_id=device(OFFSET_LIST[s], -1), device_id_type=pl.DeviceIdType.MESH
             )
 
-    basis_copy = pltpu.make_async_copy(bases_ref, basis, basis_sem)
-    basis_copy.start()
     block_copies = [
         pltpu.make_async_copy(couplings_ref.at[s], blocks.at[s], block_sem.at[s]) for s in range(count)
     ]
@@ -197,8 +200,10 @@
 
     tall = min(512, m)
 
-    def apply(slot, n):
+    def apply(slot, n, more=None):
         piece = sent[slot][n][1]
+        if more is not None:
+            piece = pl.ds(piece.start, piece.size + sent[slot][more][1].size)
 
         @pl.when(up[slot])
         def _():
@@ -225,6 +230,14 @@
             back_out[slot] = out
             back_copies[slot].start()
 
+    even = place[2] % 2 == 0
+
+    def finish(slot, n, more=None):
+        arrived(slot, n)
+        if more is not None:
+            arrived(slot, more)
+        apply(slot, n, more)
+
     arrived(Z, 0)
     apply(Z, 0)
     arrived(X, 0)
@@ -232,30 +245,31 @@
     start(XZ, 0)
     arrived(Y, 1)
     start(XY, 1)
+    late = jnp.logical_and(down[XZ], place[2] % 2 == 0)
+    pl.when(jnp.logical_and(last[2], jnp.logical_not(late)))(last[0].start)
     arrived(Z, 1)
     apply(Z, 1)
     apply(X, 0)
     apply(Y, 1)
     project(Z)
-    arrived(XZ, 0)
-    apply(XZ, 0)
     project(Y)
+    pl.when(even)(lambda: finish(XZ, 0))
     project(X)
     arrived(X, 1)
     start(XZ, 1)
     arrived(Y, 0)
     apply(X, 1)
     apply(Y, 0)
-    arrived(XZ, 1)
-    apply(XZ, 1)
     project(XY)
-    for n in (0, 2):
-        arrived(XY, n)
-        apply(XY, n)
+    pl.when(jnp.logical_not(even))(lambda: finish(XZ, 0))
+    pl.when(even)(lambda: finish(XZ, 1))
     project(XZ)
-    for n in (1, 3):
-        arrived(XY, n)
-        apply(XY, n)
+    pl.when(jnp.logical_and(last[2], late))(last[0].start)
+    finish(XY, 0)
+    finish(XY, 2)
+    pl.when(jnp.logical_not(even))(lambda: finish(XZ, 1))
+    finish(XY, 1)
+    finish(XY, 3, 4)
     for s in range(count):
         pl.when(up[s])(back_copies[s].wait_recv)
     for s in range(count):
@@ -309,8 +323,8 @@
                 pltpu.SemaphoreType.REGULAR((count,)),
                 dma,
                 dma((count,)),
-                dma((count, 4)),
-                dma((count, 4)),
+                dma((count, 5)),
+                dma((count, 5)),
                 dma((count, 2)),
                 dma((count, 2)),
                 dma((2,)),
@@ -325,6 +339,14 @@
             couplings.reshape(count, m, m),
             vectors.reshape(m, r),
         )
+        projected, applied = pl.pallas_call(
+            writer,
+            out_shape=(jax.ShapeDtypeStruct(projected.shape, f32), jax.ShapeDtypeStruct(applied.shape, f32)),
+            in_specs=[pl.BlockSpec(memory_space=pltpu.VMEM)] * 2,
+            out_specs=(pl.BlockSpec(memory_space=pltpu.HBM),) * 2,
+            scratch_shapes=[dma((2,))],
+            compiler_params=pltpu.CompilerParams(vmem_limit_bytes=8 << 20),
+        )(projected, applied)
         return (
             projected.reshape(1, 1, 1, count, k, k),
             applied.reshape(1, 1, 1, m, r),

time: 46.1 us -> 44.6 us (0.967)
  local copies, waits for them, and re-layouts: 1.7 us -> 0 us
    unnamed x2 -> x0, local copies, waits for them, and re-layouts: 1.7 us -> none
    pallas_call x0 -> x1, Pallas kernels: none -> 1.1 us  [local(): pl.pallas_call(writer, out_shape=(jax.ShapeDtypeStruct(projected.shape, f...]
    pallas_call x1, Pallas kernels: 43 us -> 42.1 us  [local(): pl.pallas_call(functools.partial(kernel, sizes), out_shape=(pltpu.VMEM((c...]
where the time goes in v2:
time: 44.6 us; the launch traced here: 44.4 us
  Pallas kernels  43.2 us (97%)
  between operations  1.28 us (3%)
    pallas_call x1, Pallas kernels, local(): pl.pallas_call(functools.partial(kernel, sizes), out_shape=(pltpu.VMEM((c...  42.1 us
    pallas_call x1, Pallas kernels, local(): pl.pallas_call(writer, out_shape=(jax.ShapeDtypeStruct(projected.shape, f...  1.1 us

profile of v2, /device:TPU:0, one launch (start us, length us, event | category | flops | bytes accessed | tf_op | source)
XLA Modules:
  0.0 44.4 jit_solution(10997532156028096060)
XLA Ops:
  1.3 42.1 %shard_map.59 = (f32[5,128,128]{2,1,0:T(8,128)S(1)}, f32[1024,256]{1,0:T(8,128)S(1)}) custom-call(s32[1,1,1]{2,1,0:T(1,128)S(6)} %copy.6.ranks_ref, f32[1024,128]{1,0:T(8,128)} %bitcast.7, bf16[5,1024,1024]{2,1,0:T(8,128)(2,1)} %bitcast.5, f32[1024,256]{1,0:T(8,128)} %bitcast.6), custom_call_target="tpu_custom_call" | custom-call | tf_op jit(solution)/shard_map/pallas_call | solution.py:305
  43.4 1.1 %shard_map.60 = (f32[5,128,128]{2,1,0:T(8,128)}, f32[1024,256]{1,0:T(8,128)}) custom-call(f32[5,128,128]{2,1,0:T(8,128)S(1)} %get-tuple-element.6.projected_ref, f32[1024,256]{1,0:T(8,128)S(1)} %get-tuple-element.7.applied_ref), custom_call_target="tpu_custom_call" | custom-call | tf_op jit(solution)/shard_map/pallas_call | solution.py:342

commit v3 on v2

--- a/solution.py
+++ b/solution.py
@@ -24,7 +24,17 @@
     return jnp.dot(left, right, preferred_element_type=jnp.float32)
 
 
-def kernel(
+def kernel(sizes, *refs):
+    dma = pltpu.SemaphoreType.DMA
+    count = refs[2].shape[0]
+    pl.run_scoped(
+        functools.partial(body, sizes, *refs),
+        pltpu.SemaphoreType.REGULAR, dma, dma((count,)), dma((12,)), dma((12,)), dma((count + 1,)), dma((count + 1,)),
+        dma((2,)), dma((2,)), dma((count,)), dma((count,)),
+    )
+
+
+def body(
     sizes, ranks_ref, bases_ref, couplings_ref, vectors_ref, projected_ref, applied_ref,
     basis, stacked, basis_parts, blocks, values, left_out, left_in, relay, back_out,
     ready, basis_sem, block_sem, value_send, value_recv, left_send, left_recv, relay_send, relay_recv,
@@ -55,6 +65,7 @@
 
     barrier = pltpu.get_barrier_semaphore()
     partners = jnp.int32(0)
+    senders = sum(up[s].astype(jnp.int32) for s in LEFT_SLOTS)
     for s in range(count):
         partners = partners + down[s].astype(jnp.int32)
 
@@ -78,25 +89,26 @@
         )
 
     def value_copy(slot, piece, source, offset):
+        n = sum(len(copies) for copies in sent.values())
         return remote(
-            source.at[piece], values.at[slot, piece],
-            value_send.at[slot, len(sent[slot])], value_recv.at[slot, len(sent[slot])], offset, -1,
+            source.at[piece], values.at[slot, piece], value_send.at[n], value_recv.at[n], offset, -1,
         )
 
     sent = {s: [] for s in range(count)}
 
-    def plan(slot, part, source, offset, flag, cuts=(1,)):
+    def plan(slot, part, source, offset, flag, cuts=(4,)):
         first = part * half
         for cut in cuts:
-            piece = pl.ds(first, half // cut)
+            piece = pl.ds(first, half * cut // 4)
             sent[slot].append((value_copy(slot, piece, source, offset), piece, flag, part))
-            first += half // cut
-
-    for s in (X, Y, Z):
+            first += half * cut // 4
+
+    for s in (X, Y):
         for part in (0, 1):
             plan(s, part, vectors_ref, OFFSET_LIST[s], down[s])
+    plan(Z, 0, vectors_ref, OFFSET_LIST[Z], down[Z], (8,))
     plan(XY, 0, values.at[X], OFFSET_LIST[Y], jnp.logical_and(has_up[0], has_down[1]), (2, 2))
-    plan(XY, 1, values.at[Y], OFFSET_LIST[X], jnp.logical_and(has_up[1], has_down[0]), (2, 4, 4))
+    plan(XY, 1, values.at[Y], OFFSET_LIST[X], jnp.logical_and(has_up[1], has_down[0]), (2, 1, 1))
     for part in (0, 1):
         plan(XZ, part, values.at[X], OFFSET_LIST[Z], jnp.logical_and(has_up[0], has_down[2]))
 
@@ -111,11 +123,11 @@
         pl.when(up[slot])(sent[slot][n][0].wait_recv)
 
     relays = [
-        remote(left_out.at[XY, part], relay.at[part], relay_send.at[part], relay_recv.at[part], OFFSET_LIST[s], 1)
+        remote(left_out.at[XY, part], relay.at[part], left_send.at[XY + 2 * part], relay_recv.at[part], OFFSET_LIST[s], 1)
         for part, s in ((0, X), (1, Y))
     ]
     onward = [
-        remote(relay.at[part], left_in.at[XY, part], left_send.at[XY, part], left_recv.at[XY, part], OFFSET_LIST[s], 1)
+        remote(relay.at[part], left_in.at[XY, part], relay_send.at[part], left_recv.at[XY + 2 * part], OFFSET_LIST[s], 1)
         for part, s in ((0, Y), (1, X))
     ]
     passed = (
@@ -124,7 +136,7 @@
     )
     left_copies = [
         relays if s == XY else [
-            remote(left_out.at[s], left_in.at[s], left_send.at[s, 0], left_recv.at[s, 0], OFFSET_LIST[s], 1)
+            remote(left_out.at[s], left_in.at[s], left_send.at[s], left_recv.at[s], OFFSET_LIST[s], 1)
         ]
         for s in range(count)
     ]
@@ -138,13 +150,12 @@
     start(Z, 0)
     start(X, 1)
     start(Y, 0)
-    start(Z, 1)
 
     for s in LEFT_SLOTS:
         @pl.when(down[s])
         def _():
             pl.semaphore_signal(
-                ready.at[s], inc=1, device_id=device(OFFSET_LIST[s], -1), device_id_type=pl.DeviceIdType.MESH
+                ready, inc=1, device_id=device(OFFSET_LIST[s], -1), device_id_type=pl.DeviceIdType.MESH
             )
 
     block_copies = [
@@ -163,10 +174,9 @@
     stacked[:k] = high
     stacked[k:] = low
 
-    for s in LEFT_SLOTS:
-        @pl.when(up[s])
-        def _():
-            pl.semaphore_wait(ready.at[s], 1)
+    @pl.when(senders > 0)
+    def _():
+        pl.semaphore_wait(ready, senders)
 
     for s in LEFT_ORDER:
         block_copies[s].wait()
@@ -247,8 +257,6 @@
     start(XY, 1)
     late = jnp.logical_and(down[XZ], place[2] % 2 == 0)
     pl.when(jnp.logical_and(last[2], jnp.logical_not(late)))(last[0].start)
-    arrived(Z, 1)
-    apply(Z, 1)
     apply(X, 0)
     apply(Y, 1)
     project(Z)
@@ -282,7 +290,11 @@
         pl.when(flag)(copy[1].wait_send)
 
 
-def writer(projected_ref, applied_ref, projected_out, applied_out, sems):
+def writer(*refs):
+    pl.run_scoped(functools.partial(write, *refs), pltpu.SemaphoreType.DMA((2,)))
+
+
+def write(projected_ref, applied_ref, projected_out, applied_out, sems):
     copies = [
         pltpu.make_async_copy(projected_ref, projected_out, sems.at[0]),
         pltpu.make_async_copy(applied_ref, applied_out, sems.at[1]),
@@ -301,7 +313,6 @@
         count = couplings.shape[3]
         r = vectors.shape[-1]
         f32, bf16 = jnp.float32, jnp.bfloat16
-        dma = pltpu.SemaphoreType.DMA
         projected, applied = pl.pallas_call(
             functools.partial(kernel, sizes),
             out_shape=(
@@ -320,17 +331,6 @@
                 pltpu.VMEM((count, 2, k, m // 2), f32),
                 pltpu.VMEM((2, k, m // 2), f32),
                 pltpu.VMEM((count, k, k), f32),
-                pltpu.SemaphoreType.REGULAR((count,)),
-                dma,
-                dma((count,)),
-                dma((count, 5)),
-                dma((count, 5)),
-                dma((count, 2)),
-                dma((count, 2)),
-                dma((2,)),
-                dma((2,)),
-                dma((count,)),
-                dma((count,)),
             ],
             compiler_params=pltpu.CompilerParams(collective_id=0, has_side_effects=True, vmem_limit_bytes=64000 << 10),
         )(
@@ -344,7 +344,6 @@
             out_shape=(jax.ShapeDtypeStruct(projected.shape, f32), jax.ShapeDtypeStruct(applied.shape, f32)),
             in_specs=[pl.BlockSpec(memory_space=pltpu.VMEM)] * 2,
             out_specs=(pl.BlockSpec(memory_space=pltpu.HBM),) * 2,
-            scratch_shapes=[dma((2,))],
             compiler_params=pltpu.CompilerParams(vmem_limit_bytes=8 << 20),
         )(projected, applied)
         return (

time: 44.6 us -> 43.7 us (0.980)
  Pallas kernels: 43.2 us -> 42.3 us
    pallas_call x1, Pallas kernels: 42.1 us -> 41.2 us  [local(): pl.pallas_call(functools.partial(kernel, sizes), out_shape=(pltpu.VMEM((c...]
where the time goes in v3:
time: 43.7 us; the launch traced here: 43.6 us
  Pallas kernels  42.3 us (97%)
  between operations  1.28 us (3%)
    pallas_call x1, Pallas kernels, local(): pl.pallas_call(functools.partial(kernel, sizes), out_shape=(pltpu.VMEM((c...  41.2 us
    pallas_call x1, Pallas kernels, local(): pl.pallas_call(writer, out_shape=(jax.ShapeDtypeStruct(projected.shape, f...  1.08 us

profile of v3, /device:TPU:0, one launch (start us, length us, event | category | flops | bytes accessed | tf_op | source)
XLA Modules:
  0.0 43.6 jit_solution(3049759241467758540)
XLA Ops:
  1.3 41.2 %shard_map.59 = (f32[5,128,128]{2,1,0:T(8,128)S(1)}, f32[1024,256]{1,0:T(8,128)S(1)}) custom-call(s32[1,1,1]{2,1,0:T(1,128)S(6)} %copy.6.refs_0_, f32[1024,128]{1,0:T(8,128)} %bitcast.7, bf16[5,1024,1024]{2,1,0:T(8,128)(2,1)} %bitcast.5, f32[1024,256]{1,0:T(8,128)} %bitcast.6), custom_call_target="tpu_custom_call" | custom-call | tf_op jit(solution)/shard_map/pallas_call | solution.py:316
  42.5 1.1 %shard_map.60 = (f32[5,128,128]{2,1,0:T(8,128)}, f32[1024,256]{1,0:T(8,128)}) custom-call(f32[5,128,128]{2,1,0:T(8,128)S(1)} %get-tuple-element.6.refs_0_, f32[1024,256]{1,0:T(8,128)S(1)} %get-tuple-element.7.refs_1_), custom_call_target="tpu_custom_call" | custom-call | tf_op jit(solution)/shard_map/pallas_call | solution.py:342

commit v4 on v3

--- a/solution.py
+++ b/solution.py
@@ -95,28 +95,33 @@
         )
 
     sent = {s: [] for s in range(count)}
-
-    def plan(slot, part, source, offset, flag, cuts=(4,)):
-        first = part * half
-        for cut in cuts:
-            piece = pl.ds(first, half * cut // 4)
+    quarter, eighth, shift = m // 4, m // 16, m // 64
+
+    def plan(slot, part, source, offset, flag, *cuts):
+        for first, size in cuts:
+            piece = pl.ds(first, size)
             sent[slot].append((value_copy(slot, piece, source, offset), piece, flag, part))
-            first += half * cut // 4
-
-    for s in (X, Y):
-        for part in (0, 1):
-            plan(s, part, vectors_ref, OFFSET_LIST[s], down[s])
-    plan(Z, 0, vectors_ref, OFFSET_LIST[Z], down[Z], (8,))
-    plan(XY, 0, values.at[X], OFFSET_LIST[Y], jnp.logical_and(has_up[0], has_down[1]), (2, 2))
-    plan(XY, 1, values.at[Y], OFFSET_LIST[X], jnp.logical_and(has_up[1], has_down[0]), (2, 1, 1))
+
     for part in (0, 1):
-        plan(XZ, part, values.at[X], OFFSET_LIST[Z], jnp.logical_and(has_up[0], has_down[2]))
-
-    last = sent[XY][-1]
+        plan(X, part, vectors_ref, OFFSET_LIST[X], down[X], (part * half, half))
+    plan(Y, 0, vectors_ref, OFFSET_LIST[Y], down[Y], (0, half - shift))
+    plan(Y, 1, vectors_ref, OFFSET_LIST[Y], down[Y], (half - shift, half + shift))
+    plan(Z, 0, vectors_ref, OFFSET_LIST[Z], down[Z], (0, m))
+    plan(
+        XY, 0, values.at[X], OFFSET_LIST[Y], jnp.logical_and(has_up[0], has_down[1]),
+        (0, quarter), (quarter, quarter - shift),
+    )
+    by_y = jnp.logical_and(has_up[1], has_down[0])
+    plan(XY, 1, values.at[Y], OFFSET_LIST[X], by_y, (half - shift, quarter + shift), (half + quarter, quarter - eighth))
+    plan(XY, 2, values.at[Y], OFFSET_LIST[X], by_y, (m - eighth, eighth))
+    for part in (0, 1):
+        plan(
+            XZ, part, values.at[X], OFFSET_LIST[Z], jnp.logical_and(has_up[0], has_down[2]), (part * half, half),
+        )
 
     def start(slot, part):
         for copy, _, flag, its in sent[slot]:
-            if its == part and copy is not last[0]:
+            if its == part:
                 pl.when(flag)(copy.start)
 
     def arrived(slot, n):
@@ -210,11 +215,7 @@
 
     tall = min(512, m)
 
-    def apply(slot, n, more=None):
-        piece = sent[slot][n][1]
-        if more is not None:
-            piece = pl.ds(piece.start, piece.size + sent[slot][more][1].size)
-
+    def apply(slot, piece):
         @pl.when(up[slot])
         def _():
             high, low = split2(values[slot, piece])
@@ -238,46 +239,50 @@
                 term = first[:, :k] + first[:, k:] + dot32(low, basis_parts[rows(part), :k])
                 out = term if out is None else out + term
             back_out[slot] = out
-            back_copies[slot].start()
+            if slot == X:
+                pl.when(jnp.logical_not(late))(back_copies[slot].start)
+            else:
+                back_copies[slot].start()
 
     even = place[2] % 2 == 0
-
-    def finish(slot, n, more=None):
-        arrived(slot, n)
-        if more is not None:
-            arrived(slot, more)
-        apply(slot, n, more)
-
-    arrived(Z, 0)
-    apply(Z, 0)
+    late = down[XZ]
+
+    def finish(slot, first, size, *pieces):
+        for n in pieces:
+            arrived(slot, n)
+        apply(slot, pl.ds(first, size))
+
+    finish(Z, 0, m, 0)
     arrived(X, 0)
     start(XY, 0)
     start(XZ, 0)
     arrived(Y, 1)
     start(XY, 1)
-    late = jnp.logical_and(down[XZ], place[2] % 2 == 0)
-    pl.when(jnp.logical_and(last[2], jnp.logical_not(late)))(last[0].start)
-    apply(X, 0)
-    apply(Y, 1)
+    pl.when(jnp.logical_not(late))(lambda: start(XY, 2))
+    apply(X, pl.ds(0, half))
+    apply(Y, pl.ds(half, half))
     project(Z)
     project(Y)
-    pl.when(even)(lambda: finish(XZ, 0))
+    pl.when(even)(lambda: finish(XZ, 0, half, 0))
     project(X)
     arrived(X, 1)
     start(XZ, 1)
     arrived(Y, 0)
-    apply(X, 1)
-    apply(Y, 0)
+    apply(X, pl.ds(half, half))
+    apply(Y, pl.ds(0, half))
     project(XY)
-    pl.when(jnp.logical_not(even))(lambda: finish(XZ, 0))
-    pl.when(even)(lambda: finish(XZ, 1))
+    pl.when(jnp.logical_not(even))(lambda: finish(XZ, 0, half, 0))
+    pl.when(even)(lambda: finish(XZ, half, half, 1))
     project(XZ)
-    pl.when(jnp.logical_and(last[2], late))(last[0].start)
-    finish(XY, 0)
-    finish(XY, 2)
-    pl.when(jnp.logical_not(even))(lambda: finish(XZ, 1))
-    finish(XY, 1)
-    finish(XY, 3, 4)
+    pl.when(late)(lambda: start(XY, 2))
+    pl.when(jnp.logical_and(late, down[X]))(back_copies[X].start)
+    finish(XY, 0, quarter, 0)
+    finish(XY, half, quarter, 2)
+    pl.when(jnp.logical_not(even))(lambda: finish(XZ, half, half, 1))
+    held = place[2] > 0
+    pl.when(jnp.logical_not(held))(lambda: finish(XY, half + quarter, quarter, 3, 4))
+    finish(XY, quarter, quarter, 1)
+    pl.when(held)(lambda: finish(XY, half + quarter, quarter, 3, 4))
     for s in range(count):
         pl.when(up[s])(back_copies[s].wait_recv)
     for s in range(count):

time: 43.7 us -> 43.3 us (level)
  Pallas kernels: 42.3 us -> 41.8 us
    pallas_call x1, Pallas kernels: 41.2 us -> 40.8 us  [local(): pl.pallas_call(functools.partial(kernel, sizes), out_shape=(pltpu.VMEM((c...]
where the time goes in v4:
time: 43.3 us; the launch traced here: 43.1 us
  Pallas kernels  41.8 us (97%)
  between operations  1.28 us (3%)
    pallas_call x1, Pallas kernels, local(): pl.pallas_call(functools.partial(kernel, sizes), out_shape=(pltpu.VMEM((c...  40.8 us
    pallas_call x1, Pallas kernels, local(): pl.pallas_call(writer, out_shape=(jax.ShapeDtypeStruct(projected.shape, f...  1.08 us

profile of v4, /device:TPU:0, one launch (start us, length us, event | category | flops | bytes accessed | tf_op | source)
XLA Modules:
  0.0 43.1 jit_solution(9664147494629707488)
XLA Ops:
  1.3 40.8 %shard_map.59 = (f32[5,128,128]{2,1,0:T(8,128)S(1)}, f32[1024,256]{1,0:T(8,128)S(1)}) custom-call(s32[1,1,1]{2,1,0:T(1,128)S(6)} %copy.6.refs_0_, f32[1024,128]{1,0:T(8,128)} %bitcast.7, bf16[5,1024,1024]{2,1,0:T(8,128)(2,1)} %bitcast.5, f32[1024,256]{1,0:T(8,128)} %bitcast.6), custom_call_target="tpu_custom_call" | custom-call | tf_op jit(solution)/shard_map/pallas_call | solution.py:321
  42.1 1.1 %shard_map.60 = (f32[5,128,128]{2,1,0:T(8,128)}, f32[1024,256]{1,0:T(8,128)}) custom-call(f32[5,128,128]{2,1,0:T(8,128)S(1)} %get-tuple-element.6.refs_0_, f32[1024,256]{1,0:T(8,128)S(1)} %get-tuple-element.7.refs_1_), custom_call_target="tpu_custom_call" | custom-call | tf_op jit(solution)/shard_map/pallas_call | solution.py:347

commit v5 on v4

--- a/solution.py
+++ b/solution.py
@@ -11,7 +11,6 @@
 AXES = ("gx", "gy", "gz")
 X, Y, Z, XY, XZ = range(5)
 LEFT_ORDER = (XY, Y, X, XZ, Z)
-LEFT_SLOTS = (X, Y, Z, XZ)
 
 
 def split2(value):
@@ -29,15 +28,15 @@
     count = refs[2].shape[0]
     pl.run_scoped(
         functools.partial(body, sizes, *refs),
-        pltpu.SemaphoreType.REGULAR, dma, dma((count,)), dma((12,)), dma((12,)), dma((count + 1,)), dma((count + 1,)),
-        dma((2,)), dma((2,)), dma((count,)), dma((count,)),
+        pltpu.SemaphoreType.REGULAR, pltpu.SemaphoreType.REGULAR, dma, dma((count,)), dma((12,)), dma((12,)),
+        dma((count + 1,)), dma((count + 1,)), dma((2,)), dma((2,)), dma((count,)), dma((count,)),
     )
 
 
 def body(
     sizes, ranks_ref, bases_ref, couplings_ref, vectors_ref, projected_ref, applied_ref,
     basis, stacked, basis_parts, blocks, values, left_out, left_in, relay, back_out,
-    ready, basis_sem, block_sem, value_send, value_recv, left_send, left_recv, relay_send, relay_recv,
+    ready, beyond, basis_sem, block_sem, value_send, value_recv, left_send, left_recv, relay_send, relay_recv,
     back_send, back_recv,
 ):
     count, m, k = blocks.shape[0], basis.shape[0], basis.shape[1]
@@ -63,21 +62,31 @@
     basis_copy = pltpu.make_async_copy(bases_ref, basis, basis_sem)
     basis_copy.start()
 
+    even = place[2] % 2 == 0
+    odd = jnp.logical_not(even)
+
+    def tell(flag, semaphore, offset, sign):
+        @pl.when(flag)
+        def _():
+            pl.semaphore_signal(
+                semaphore, inc=1, device_id=device(offset, sign), device_id_type=pl.DeviceIdType.MESH
+            )
+
+    def number(*flags):
+        return sum(flag.astype(jnp.int32) for flag in flags)
+
+    def hear(semaphore, amount):
+        @pl.when(amount > 0)
+        def _():
+            pl.semaphore_wait(semaphore, amount)
+
     barrier = pltpu.get_barrier_semaphore()
-    partners = jnp.int32(0)
-    senders = sum(up[s].astype(jnp.int32) for s in LEFT_SLOTS)
-    for s in range(count):
-        partners = partners + down[s].astype(jnp.int32)
-
-        @pl.when(up[s])
-        def _():
-            pl.semaphore_signal(
-                barrier, inc=1, device_id=device(OFFSET_LIST[s], 1), device_id_type=pl.DeviceIdType.MESH
-            )
-
-    @pl.when(partners > 0)
-    def _():
-        pl.semaphore_wait(barrier, partners)
+    along_x, along_y, along_z = (OFFSET_LIST[s] for s in (X, Y, Z))
+    tell(up[X], barrier, along_x, 1)
+    tell(up[Y], barrier, along_y, 1)
+    tell(jnp.logical_and(odd, up[Z]), barrier, along_z, 1)
+    tell(jnp.logical_and(odd, down[Z]), barrier, along_z, -1)
+    hear(barrier, number(down[X], down[Y], jnp.logical_and(even, down[Z]), jnp.logical_and(even, up[Z])))
 
     def rows(part):
         return pl.ds(part * half, half)
@@ -152,16 +161,13 @@
 
     start(X, 0)
     start(Y, 1)
-    start(Z, 0)
+    pl.when(even)(lambda: start(Z, 0))
     start(X, 1)
     start(Y, 0)
-
-    for s in LEFT_SLOTS:
-        @pl.when(down[s])
-        def _():
-            pl.semaphore_signal(
-                ready, inc=1, device_id=device(OFFSET_LIST[s], -1), device_id_type=pl.DeviceIdType.MESH
-            )
+    tell(down[X], ready, along_x, -1)
+    tell(down[Y], ready, along_y, -1)
+    tell(jnp.logical_and(even, down[Z]), ready, along_z, -1)
+    tell(jnp.logical_and(even, up[Z]), ready, along_z, 1)
 
     block_copies = [
         pltpu.make_async_copy(couplings_ref.at[s], blocks.at[s], block_sem.at[s]) for s in range(count)
@@ -179,9 +185,9 @@
     stacked[:k] = high
     stacked[k:] = low
 
-    @pl.when(senders > 0)
-    def _():
-        pl.semaphore_wait(ready, senders)
+    hear(ready, number(up[X], up[Y], jnp.logical_and(odd, up[Z]), jnp.logical_and(odd, down[Z])))
+    tell(jnp.logical_and(down[Z], up[X]), beyond, along_z, -1)
+    pl.when(odd)(lambda: start(Z, 0))
 
     for s in LEFT_ORDER:
         block_copies[s].wait()
@@ -211,7 +217,10 @@
             copy[0].wait_recv()
             copy[1].start()
 
-    pl.when(up[XZ])(left_copies[XZ][0].start)
+    @pl.when(up[XZ])
+    def _():
+        pl.semaphore_wait(beyond, 1)
+        left_copies[XZ][0].start()
 
     tall = min(512, m)
 
@@ -244,7 +253,6 @@
             else:
                 back_copies[slot].start()
 
-    even = place[2] % 2 == 0
     late = down[XZ]
 
     def finish(slot, first, size, *pieces):
@@ -271,14 +279,14 @@
     apply(X, pl.ds(half, half))
     apply(Y, pl.ds(0, half))
     project(XY)
-    pl.when(jnp.logical_not(even))(lambda: finish(XZ, 0, half, 0))
+    pl.when(odd)(lambda: finish(XZ, 0, half, 0))
     pl.when(even)(lambda: finish(XZ, half, half, 1))
     project(XZ)
     pl.when(late)(lambda: start(XY, 2))
     pl.when(jnp.logical_and(late, down[X]))(back_copies[X].start)
     finish(XY, 0, quarter, 0)
     finish(XY, half, quarter, 2)
-    pl.when(jnp.logical_not(even))(lambda: finish(XZ, half, half, 1))
+    pl.when(odd)(lambda: finish(XZ, half, half, 1))
     held = place[2] > 0
     pl.when(jnp.logical_not(held))(lambda: finish(XY, half + quarter, quarter, 3, 4))
     finish(XY, quarter, quarter, 1)

time: 43.3 us -> 42.7 us (0.986)
  Pallas kernels: 41.8 us -> 41.2 us
    pallas_call x1, Pallas kernels: 40.8 us -> 40.1 us  [local(): pl.pallas_call(functools.partial(kernel, sizes), out_shape=(pltpu.VMEM((c...]
where the time goes in v5:
time: 42.7 us; the launch traced here: 42.5 us
  Pallas kernels  41.2 us (96%)
  between operations  1.28 us (3%)
    pallas_call x1, Pallas kernels, local(): pl.pallas_call(functools.partial(kernel, sizes), out_shape=(pltpu.VMEM((c...  40.1 us
    pallas_call x1, Pallas kernels, local(): pl.pallas_call(writer, out_shape=(jax.ShapeDtypeStruct(projected.shape, f...  1.08 us

profile of v5, /device:TPU:0, one launch (start us, length us, event | category | flops | bytes accessed | tf_op | source)
XLA Modules:
  0.0 42.5 jit_solution(13949919796962664687)
XLA Ops:
  1.3 40.1 %shard_map.59 = (f32[5,128,128]{2,1,0:T(8,128)S(1)}, f32[1024,256]{1,0:T(8,128)S(1)}) custom-call(s32[1,1,1]{2,1,0:T(1,128)S(6)} %copy.6.refs_0_, f32[1024,128]{1,0:T(8,128)} %bitcast.7, bf16[5,1024,1024]{2,1,0:T(8,128)(2,1)} %bitcast.5, f32[1024,256]{1,0:T(8,128)} %bitcast.6), custom_call_target="tpu_custom_call" | custom-call | tf_op jit(solution)/shard_map/pallas_call | solution.py:329
  41.4 1.1 %shard_map.60 = (f32[5,128,128]{2,1,0:T(8,128)}, f32[1024,256]{1,0:T(8,128)}) custom-call(f32[5,128,128]{2,1,0:T(8,128)S(1)} %get-tuple-element.6.refs_0_, f32[1024,256]{1,0:T(8,128)S(1)} %get-tuple-element.7.refs_1_), custom_call_target="tpu_custom_call" | custom-call | tf_op jit(solution)/shard_map/pallas_call | solution.py:355

commit v6 on v5

--- a/solution.py
+++ b/solution.py
@@ -262,7 +262,7 @@
 
     finish(Z, 0, m, 0)
     arrived(X, 0)
-    start(XY, 0)
+    pl.when(even)(lambda: start(XY, 0))
     start(XZ, 0)
     arrived(Y, 1)
     start(XY, 1)
@@ -270,13 +270,19 @@
     apply(X, pl.ds(0, half))
     apply(Y, pl.ds(half, half))
     project(Z)
-    project(Y)
+    pl.when(even)(lambda: project(Y))
     pl.when(even)(lambda: finish(XZ, 0, half, 0))
     project(X)
     arrived(X, 1)
     start(XZ, 1)
     arrived(Y, 0)
     apply(X, pl.ds(half, half))
+
+    @pl.when(odd)
+    def _():
+        start(XY, 0)
+        project(Y)
+
     apply(Y, pl.ds(0, half))
     project(XY)
     pl.when(odd)(lambda: finish(XZ, 0, half, 0))
@@ -287,7 +293,7 @@
     finish(XY, 0, quarter, 0)
     finish(XY, half, quarter, 2)
     pl.when(odd)(lambda: finish(XZ, half, half, 1))
-    held = place[2] > 0
+    held = jnp.logical_and(place[2] > 0, even)
     pl.when(jnp.logical_not(held))(lambda: finish(XY, half + quarter, quarter, 3, 4))
     finish(XY, quarter, quarter, 1)
     pl.when(held)(lambda: finish(XY, half + quarter, quarter, 3, 4))

time: 42.7 us -> 42.6 us (level)
  no operation moved by 1% of the time
where the time goes in v6:
time: 42.6 us; the launch traced here: 42.2 us
  Pallas kernels  41 us (96%)
  between operations  1.28 us (3%)
    pallas_call x1, Pallas kernels, local(): pl.pallas_call(functools.partial(kernel, sizes), out_shape=(pltpu.VMEM((c...  39.9 us
    pallas_call x1, Pallas kernels, local(): pl.pallas_call(writer, out_shape=(jax.ShapeDtypeStruct(projected.shape, f...  1.08 us

profile of v6, /device:TPU:0, one launch (start us, length us, event | category | flops | bytes accessed | tf_op | source)
XLA Modules:
  0.0 42.2 jit_solution(357220719506658660)
XLA Ops:
  1.3 39.9 %shard_map.59 = (f32[5,128,128]{2,1,0:T(8,128)S(1)}, f32[1024,256]{1,0:T(8,128)S(1)}) custom-call(s32[1,1,1]{2,1,0:T(1,128)S(6)} %copy.6.refs_0_, f32[1024,128]{1,0:T(8,128)} %bitcast.7, bf16[5,1024,1024]{2,1,0:T(8,128)(2,1)} %bitcast.5, f32[1024,256]{1,0:T(8,128)} %bitcast.6), custom_call_target="tpu_custom_call" | custom-call | tf_op jit(solution)/shard_map/pallas_call | solution.py:335
  41.2 1.1 %shard_map.60 = (f32[5,128,128]{2,1,0:T(8,128)}, f32[1024,256]{1,0:T(8,128)}) custom-call(f32[5,128,128]{2,1,0:T(8,128)S(1)} %get-tuple-element.6.refs_0_, f32[1024,256]{1,0:T(8,128)S(1)} %get-tuple-element.7.refs_1_), custom_call_target="tpu_custom_call" | custom-call | tf_op jit(solution)/shard_map/pallas_call | solution.py:361

commit v7 on v6

--- a/solution.py
+++ b/solution.py
@@ -60,7 +60,6 @@
         return {name: p + sign * o for name, p, o in zip(AXES, place, offset)}
 
     basis_copy = pltpu.make_async_copy(bases_ref, basis, basis_sem)
-    basis_copy.start()
 
     even = place[2] % 2 == 0
     odd = jnp.logical_not(even)
@@ -161,6 +160,7 @@
 
     start(X, 0)
     start(Y, 1)
+    basis_copy.start()
     pl.when(even)(lambda: start(Z, 0))
     start(X, 1)
     start(Y, 0)
@@ -315,8 +315,8 @@
 
 def write(projected_ref, applied_ref, projected_out, applied_out, sems):
     copies = [
-        pltpu.make_async_copy(projected_ref, projected_out, sems.at[0]),
-        pltpu.make_async_copy(applied_ref, applied_out, sems.at[1]),
+        pltpu.make_async_copy(applied_ref, applied_out, sems.at[0]),
+        pltpu.make_async_copy(projected_ref, projected_out, sems.at[1]),
     ]
     for copy in copies:
         copy.start()

time: 42.6 us -> 42.6 us (level)
  no operation moved by 1% of the time
where the time goes in v7:
time: 42.6 us; the launch traced here: 42.2 us
  Pallas kernels  41 us (96%)
  between operations  1.28 us (3%)
    pallas_call x1, Pallas kernels, local(): pl.pallas_call(functools.partial(kernel, sizes), out_shape=(pltpu.VMEM((c...  39.9 us
    pallas_call x1, Pallas kernels, local(): pl.pallas_call(writer, out_shape=(jax.ShapeDtypeStruct(projected.shape, f...  1.07 us

profile of v7, /device:TPU:0, one launch (start us, length us, event | category | flops | bytes accessed | tf_op | source)
XLA Modules:
  0.0 42.2 jit_solution(2787294795082919780)
XLA Ops:
  1.3 39.9 %shard_map.59 = (f32[5,128,128]{2,1,0:T(8,128)S(1)}, f32[1024,256]{1,0:T(8,128)S(1)}) custom-call(s32[1,1,1]{2,1,0:T(1,128)S(6)} %copy.6.refs_0_, f32[1024,128]{1,0:T(8,128)} %bitcast.7, bf16[5,1024,1024]{2,1,0:T(8,128)(2,1)} %bitcast.5, f32[1024,256]{1,0:T(8,128)} %bitcast.6), custom_call_target="tpu_custom_call" | custom-call | tf_op jit(solution)/shard_map/pallas_call | solution.py:335
  41.2 1.1 %shard_map.60 = (f32[5,128,128]{2,1,0:T(8,128)}, f32[1024,256]{1,0:T(8,128)}) custom-call(f32[5,128,128]{2,1,0:T(8,128)S(1)} %get-tuple-element.6.refs_0_, f32[1024,256]{1,0:T(8,128)S(1)} %get-tuple-element.7.refs_1_), custom_call_target="tpu_custom_call" | custom-call | tf_op jit(solution)/shard_map/pallas_call | solution.py:361
